TPU v7x, 32 devices: a whole 2x2x4 slice. The times are simulated.
32 devices in a mesh: facet: 4 (over z), chan: 8 (over y, x, core).
Axes of the slice: x: 2, y: 2, z: 4, core: 2. Of those that a mesh axis runs over, the one named last changes fastest.
Arguments:
- visibilities: bfloat16 [2, 8, 256, 32, 128], P(None, None, None, ('facet', 'chan')), may hold values from -12 to 12
- kernels: bfloat16 [32, 256, 512], replicated, may hold values from -0.25 to 0.25
- delays: float32 [8, 256, 128], P('facet'), may hold values from -4 to 4
- tile_of: int32 [8, 256], P('facet'), may hold values from 0 to 127
- plane_of: int32 [8, 256], P('facet'), may hold values from 0 to 31
- counts: int32 [8], P('facet'), may hold values from 64 to 256
- neighbours: int32 [8, 4], replicated, may hold values from 0 to 7, as said below
Outputs:
- joined_grids: float32 [128, 8, 4, 512], P('chan', 'facet')
Inputs may be any that keep to these rules, and one draw needn't show every extreme that they name: `neighbours`: each row names 4 different facets, none of them its own.
All inputs are finite; a program needn't handle non-finite values.
Results may differ from a plain program's by a relative error of at most 0.0043.
Values may be sent and summed in bfloat16 or wider, within the bound.
A program may use at most 128 MiB of HBM per device.

v0:
```python
import functools
import math

import jax
import jax.numpy as jnp
from jax import lax
from jax.experimental import pallas as pl
from jax.experimental.pallas import tpu as pltpu
from jax.sharding import PartitionSpec as P

AVG = 8
TS = 16
NT_DEV = 16
EDGE = 4
LANES = 128
JOINED = 3
ORDER = (3, 0, 1, 2)
MESH = pl.DeviceIdType.MESH


def series(first, count, scale):
    return [
        (-1.0) ** i * scale ** (2 * i + first) / math.factorial(2 * i + first)
        for i in range(count)
    ]


SIN_HALF = series(1, 7, math.pi)
COS_HALF = series(0, 7, math.pi)


def turn_parts(turns):
    frac = turns - jnp.round(turns)
    square = frac * frac
    sine = jnp.full_like(frac, SIN_HALF[-1])
    cosine = jnp.full_like(frac, COS_HALF[-1])
    for a, b in zip(SIN_HALF[-2::-1], COS_HALF[-2::-1]):
        sine = sine * square + a
        cosine = cosine * square + b
    sine = sine * frac
    return 1.0 - 2.0 * sine * sine, 2.0 * sine * cosine


def flip(index, mask):
    bit = 1
    while bit <= mask:
        if mask & bit:
            index = index + bit - 2 * bit * lax.rem(index // bit, 2)
        bit *= 2
    return index


def kernel(
    cfg,
    neigh_ref,
    count_ref,
    vis_ref,
    delay_ref,
    tile_ref,
    plane_ref,
    kern_ref,
    out_ref,
    pair,
    part,
    got,
    raw,
    wide,
    rough,
    turns,
    codes,
    rows,
    kern,
    lhs,
    grid,
    final,
    mate_send,
    mate_recv,
    rough_send,
    rough_recv,
    turn_send,
    turn_recv,
    code_send,
    code_recv,
    part_send,
    part_recv,
    raw_send,
    raw_recv,
    row_send,
    row_recv,
    relay_send,
    relay_recv,
    fin_send,
    fin_recv,
    own_sem,
    kern_sem,
):
    n, nz, facets, fac, blk, groups, planes, tiles, joined, order = cfg
    me = lax.axis_index("chan")
    zme = lax.axis_index("facet")
    channels = groups * AVG * nz
    tile = kern_ref.shape[1] // 2
    edge = EDGE * TS
    pairs = n // 2
    parity = lax.rem(me, 2)
    mate = me + 1 - 2 * parity
    my_pair = me // 2
    half_avg = AVG // 2
    chunk_z = [flip(zme, c) for c in range(nz)]

    def group_of(c):
        return pl.ds(chunk_z[c] * fac, fac)

    load_kern = pltpu.make_async_copy(kern_ref, kern, kern_sem)
    own_wide = pltpu.make_async_copy(delay_ref.at[:, :, parity], wide, own_sem.at[nz])
    own_turns = pltpu.make_async_copy(
        delay_ref.at[:, my_pair, parity], turns.at[zme], own_sem.at[nz + 1]
    )

    def own_copy(c):
        if c >= joined:
            return pltpu.make_async_copy(
                vis_ref.at[:, group_of(c), my_pair, parity],
                raw.at[me, :, group_of(c)],
                own_sem.at[c],
            )
        return pltpu.make_async_copy(
            vis_ref.at[:, group_of(c), :, parity],
            pair.at[parity, :, group_of(c)],
            own_sem.at[c],
        )

    barrier = pltpu.get_barrier_semaphore()
    for d in range(1, n):
        pl.semaphore_signal(
            barrier, inc=1, device_id={"chan": lax.rem(me + d, n)}, device_id_type=MESH
        )
    for d in range(1, nz):
        pl.semaphore_signal(
            barrier, inc=1, device_id={"facet": chunk_z[d]}, device_id_type=MESH
        )
    own_wide.start()
    for c in range(nz):
        own_copy(c).start()
    own_turns.start()
    load_kern.start()

    blocks = blk * n
    block_id = lax.broadcasted_iota(jnp.int32, (1, blocks), 1)
    for i in range(fac):
        codes[zme, i : i + 1] = jnp.where(
            block_id < count_ref[i],
            plane_ref[i : i + 1] * tiles + tile_ref[i : i + 1],
            -1,
        )
    own_wide.wait()
    rough[zme] = wide[...].astype(jnp.bfloat16)
    pl.semaphore_wait(barrier, n + nz - 2)

    def mate_copy(c, slot):
        return pltpu.make_async_remote_copy(
            src_ref=vis_ref.at[:, group_of(c), :, 1 - parity],
            dst_ref=pair.at[slot, :, group_of(c)],
            send_sem=mate_send.at[c],
            recv_sem=mate_recv.at[c],
            device_id={"chan": mate},
            device_id_type=MESH,
        )

    def facet_copy(src, buffer, slot, d, send, recv):
        return pltpu.make_async_remote_copy(
            src_ref=src,
            dst_ref=buffer.at[slot],
            send_sem=send.at[d],
            recv_sem=recv.at[d],
            device_id={"facet": chunk_z[d]},
            device_id_type=MESH,
        )

    def rough_copy(d, slot):
        return facet_copy(rough.at[zme], rough, slot, d, rough_send, rough_recv)

    def turn_copy(d, slot):
        return facet_copy(
            delay_ref.at[:, my_pair, parity], turns, slot, d, turn_send, turn_recv
        )

    def code_copy(d, slot):
        return facet_copy(codes.at[zme], codes, slot, d, code_send, code_recv)

    def raw_copy(c, d, slot):
        peer = lax.rem(me + d, n)
        return pltpu.make_async_remote_copy(
            src_ref=vis_ref.at[:, group_of(c), peer // 2, lax.rem(peer, 2)],
            dst_ref=raw.at[slot, :, group_of(c)],
            send_sem=raw_send.at[d, c],
            recv_sem=raw_recv.at[d, c],
            device_id={"chan": peer},
            device_id_type=MESH,
        )

    for c in range(joined):
        mate_copy(c, parity).start()
    for c in order:
        if 0 < c < joined:
            rough_copy(c, zme).start()
        if c:
            turn_copy(c, zme).start()
        if c >= joined:
            for d in range(1, n):
                raw_copy(c, d, me).start()
    for d in range(1, nz):
        code_copy(d, zme).start()

    my_blocks = pl.ds(pl.multiple_of(me * blk, blk), blk)

    def part_copy(c, d, owner, slot):
        return pltpu.make_async_remote_copy(
            src_ref=part.at[owner, :, group_of(c)],
            dst_ref=got.at[slot, :, group_of(c)],
            send_sem=part_send.at[d, c],
            recv_sem=part_recv.at[d, c],
            device_id={"chan": 2 * owner + parity},
            device_id_type=MESH,
        )

    def row_copy(owner, peer, c, send, recv):
        piece = rows.at[group_of(c), pl.ds(pl.multiple_of(owner * blk, blk), blk)]
        return pltpu.make_async_remote_copy(
            src_ref=piece,
            dst_ref=piece,
            send_sem=send,
            recv_sem=recv,
            device_id={"chan": peer},
            device_id_type=MESH,
        )

    def after(d):
        return lax.rem(my_pair + d, pairs)

    def before(d):
        return lax.rem(my_pair + pairs - d, pairs)

    def join_pair(c):
        if c >= joined:
            return
        own_copy(c).wait()
        mate_copy(c, 1 - parity).wait_recv()
        if c:
            rough_copy(c, chunk_z[c]).wait_recv()

        def one(i, carry):
            slot = i // pairs
            q = lax.rem(i, pairs)
            f = chunk_z[c] * fac + slot
            delay = rough[chunk_z[c], slot, q].astype(jnp.float32) if c else wide[slot, q]
            cosine, sine = turn_parts(delay * (0.5 / channels))
            real = pair[1, 0, f, q].astype(jnp.float32)
            imag = pair[1, 1, f, q].astype(jnp.float32)
            part[q, 0, f] = (
                pair[0, 0, f, q].astype(jnp.float32) + (real * cosine - imag * sine)
            ).astype(jnp.bfloat16)
            part[q, 1, f] = (
                pair[0, 1, f, q].astype(jnp.float32) + (real * sine + imag * cosine)
            ).astype(jnp.bfloat16)
            return carry

        lax.fori_loop(0, fac * pairs, one, 0)
        for d in range(1, pairs):
            part_copy(c, d, after(d), my_pair).start()
        got[my_pair, :, group_of(c)] = part[my_pair, :, group_of(c)]

    def rotate(c):
        if c:
            turn_copy(c, chunk_z[c]).wait_recv()
        else:
            own_turns.wait()
        if c < joined:
            for d in range(1, pairs):
                part_copy(c, d, after(d), before(d)).wait_recv()
            source, terms = got, half_avg
        else:
            own_copy(c).wait()
            for d in range(1, n):
                raw_copy(c, d, lax.rem(me + n - d, n)).wait_recv()
            source, terms = raw, AVG
        step_turns = 0.5 * AVG / (terms * channels)

        def one(i, carry):
            f = chunk_z[c] * fac + i
            delay = turns[chunk_z[c], i]
            step_cos, step_sin = turn_parts(delay * step_turns)
            for g in range(groups):
                first = (zme * groups + g) * AVG
                start_cos, start_sin = turn_parts(
                    delay * (1.0 + (0.5 / channels) * first.astype(jnp.float32))
                )
                top = (g + 1) * terms - 1
                real = source[top, 0, f].astype(jnp.float32)
                imag = source[top, 1, f].astype(jnp.float32)
                for k in range(top - 1, g * terms - 1, -1):
                    next_real = source[k, 0, f].astype(jnp.float32) + (
                        real * step_cos - imag * step_sin
                    )
                    imag = source[k, 1, f].astype(jnp.float32) + (
                        real * step_sin + imag * step_cos
                    )
                    real = next_real
                rows[f, my_blocks, 2 * LANES * g : 2 * LANES * g + LANES] = (
                    (real * start_cos - imag * start_sin) * (1.0 / AVG)
                ).astype(jnp.bfloat16)
                rows[f, my_blocks, 2 * LANES * g + LANES : 2 * LANES * (g + 1)] = (
                    (real * start_sin + imag * start_cos) * (1.0 / AVG)
                ).astype(jnp.bfloat16)
            return carry

        lax.fori_loop(0, fac, one, 0)
        for q in range(1, pairs):
            row_copy(me, 2 * after(q) + parity, c, row_send.at[q, c], row_recv.at[q, c]).start()
        row_copy(me, mate, c, row_send.at[0, c], row_recv.at[0, c]).start()

    def relay(c):
        for q in range(1, pairs):
            owner = 2 * before(q) + parity
            row_copy(owner, mate, c, row_send.at[q, c], row_recv.at[q, c]).wait_recv()
            row_copy(owner, mate, c, relay_send.at[q, c], relay_recv.at[q, c]).start()

    entry = lax.broadcasted_iota(jnp.int32, (planes * NT_DEV, blocks), 0)
    wanted = (entry // NT_DEV) * tiles + me * NT_DEV + lax.rem(entry, NT_DEV)

    def gather_rows(c):
        if c:
            code_copy(c, chunk_z[c]).wait_recv()
        row_copy(mate, mate, c, row_send.at[0, c], row_recv.at[0, c]).wait_recv()
        for q in range(1, pairs):
            owner = 2 * before(q) + 1 - parity
            row_copy(owner, mate, c, relay_send.at[q, c], relay_recv.at[q, c]).wait_recv()
        for i in range(fac):
            f = chunk_z[c] * fac + i
            code = codes[chunk_z[c], i : i + 1]
            table = (code == wanted).astype(jnp.float32).astype(jnp.bfloat16)
            summed = jnp.dot(table, rows[f], preferred_element_type=jnp.float32).astype(
                jnp.bfloat16
            )
            for g in range(groups):
                at = pl.ds(pl.multiple_of((g * facets + f) * NT_DEV, NT_DEV), NT_DEV)
                for p in range(planes):
                    lhs[at, 2 * LANES * p : 2 * LANES * (p + 1)] = summed[
                        p * NT_DEV : (p + 1) * NT_DEV, 2 * LANES * g : 2 * LANES * (g + 1)
                    ]

    stages = (join_pair, rotate, relay, gather_rows)
    for step in range(nz + len(stages) - 1):
        for lag, stage in enumerate(stages):
            if 0 <= step - lag < nz:
                stage(order[step - lag])

    span = facets * NT_DEV
    row_id = lax.broadcasted_iota(jnp.int32, (NT_DEV, span), 0)
    col_id = lax.broadcasted_iota(jnp.int32, (NT_DEV, span), 1)
    same_tile = lax.rem(col_id, NT_DEV) == row_id
    col_facet = col_id // NT_DEV
    weights = []
    for f in range(facets):
        weight = jnp.zeros((NT_DEV, span), jnp.float32)
        for k in range(neigh_ref.shape[0]):
            weight += jnp.where(same_tile & (col_facet == neigh_ref[k, f]), 0.25, 0.0)
        weights.append(weight)
    mix = jnp.concatenate(weights, axis=0).astype(jnp.bfloat16)
    keep = lax.broadcasted_iota(jnp.int32, (span, LANES), 1) >= LANES - edge

    def fin_copy(half, d, slot):
        return pltpu.make_async_remote_copy(
            src_ref=final.at[half, chunk_z[d]],
            dst_ref=out_ref.at[slot, :, :, pl.ds(half * tile, tile)],
            send_sem=fin_send.at[d, half],
            recv_sem=fin_recv.at[d, half],
            device_id={"facet": chunk_z[d]},
            device_id_type=MESH,
        )

    load_kern.wait()
    for half in range(2):
        grid[...] = jnp.dot(
            lhs[...],
            kern[:, half * tile : (half + 1) * tile],
            preferred_element_type=jnp.float32,
        )
        for g in range(groups):
            here = slice(g * span, (g + 1) * span)
            blended = jnp.dot(
                mix, grid[here, :LANES].astype(jnp.bfloat16), preferred_element_type=jnp.float32
            )
            moved = pltpu.roll(blended, LANES - edge, 1)
            grid[here, tile - LANES :] += jnp.where(keep, moved, 0.0)
        for z in range(nz):
            for g in range(groups):
                at = (g * facets + z * fac) * NT_DEV
                final[half, z, g] = grid[at : at + fac * NT_DEV].astype(jnp.bfloat16)
        for d in range(1, nz):
            fin_copy(half, d, zme).start()
        out_ref[zme, :, :, half * tile : (half + 1) * tile] = final[half, zme]

    for c in range(nz):
        if c < joined:
            mate_copy(c, parity).wait_send()
            for d in range(1, pairs):
                part_copy(c, d, after(d), my_pair).wait_send()
        else:
            for d in range(1, n):
                raw_copy(c, d, me).wait_send()
        for q in range(pairs):
            row_copy(me, mate, c, row_send.at[q, c], row_recv.at[q, c]).wait_send()
        for q in range(1, pairs):
            row_copy(me, mate, c, relay_send.at[q, c], relay_recv.at[q, c]).wait_send()
    for d in range(1, nz):
        turn_copy(d, zme).wait_send()
        if d < joined:
            rough_copy(d, zme).wait_send()
        code_copy(d, zme).wait_send()
    for half in range(2):
        for d in range(1, nz):
            fin_copy(half, d, zme).wait_send()
            fin_copy(half, d, chunk_z[d]).wait_recv()


def local(visibilities, kernels, delays, tile_of, plane_of, counts, neighbours):
    n = lax.axis_size("chan")
    nz = lax.axis_size("facet")
    halves, facets, blocks, ch_dev, lanes = visibilities.shape
    planes, depth, cells = kernels.shape
    fac = facets // nz
    blk = blocks // n
    pairs = n // 2
    groups = n * ch_dev // AVG
    tiles = NT_DEV * n
    vis = visibilities.reshape(halves, facets, pairs, 2, blk, lanes)
    joined = min(JOINED, nz)
    order = ORDER if nz == len(ORDER) else tuple(range(nz))
    cfg = (n, nz, facets, fac, blk, groups, planes, tiles, joined, order)
    dma = pltpu.SemaphoreType.DMA
    span = facets * NT_DEV
    smem = pl.BlockSpec(memory_space=pltpu.SMEM)
    vmem = pl.BlockSpec(memory_space=pltpu.VMEM)
    anywhere = pl.BlockSpec(memory_space=pl.ANY)
    out = pl.pallas_call(
        functools.partial(kernel, cfg),
        out_shape=jax.ShapeDtypeStruct((nz, groups, fac * NT_DEV, cells), jnp.bfloat16),
        in_specs=[smem, smem, anywhere, anywhere, vmem, vmem, anywhere],
        out_specs=vmem,
        scratch_shapes=[
            pltpu.VMEM((2, halves, facets, pairs, blk, lanes), jnp.bfloat16),
            pltpu.VMEM((pairs, halves, facets, blk, lanes), jnp.bfloat16),
            pltpu.VMEM((pairs, halves, facets, blk, lanes), jnp.bfloat16),
            pltpu.VMEM((n, halves, facets, blk, lanes), jnp.bfloat16),
            pltpu.VMEM((fac, pairs, blk, lanes), jnp.float32),
            pltpu.VMEM((nz, fac, pairs, blk, lanes), jnp.bfloat16),
            pltpu.VMEM((nz, fac, blk, lanes), jnp.float32),
            pltpu.VMEM((nz, fac, blocks), jnp.int32),
            pltpu.VMEM((facets, blocks, groups * depth), jnp.bfloat16),
            pltpu.VMEM((planes * depth, cells), jnp.bfloat16),
            pltpu.VMEM((groups * span, planes * depth), jnp.bfloat16),
            pltpu.VMEM((groups * span, cells // 2), jnp.float32),
            pltpu.VMEM((2, nz, groups, fac * NT_DEV, cells // 2), jnp.bfloat16),
            dma((nz,)),
            dma((nz,)),
            dma((nz,)),
            dma((nz,)),
            dma((nz,)),
            dma((nz,)),
            dma((nz,)),
            dma((nz,)),
            dma((pairs, nz)),
            dma((pairs, nz)),
            dma((n, nz)),
            dma((n, nz)),
            dma((pairs, nz)),
            dma((pairs, nz)),
            dma((pairs, nz)),
            dma((pairs, nz)),
            dma((nz, 2)),
            dma((nz, 2)),
            dma((nz + 2,)),
            dma,
        ],
        compiler_params=pltpu.CompilerParams(
            collective_id=0, has_side_effects=True, vmem_limit_bytes=60 * 1024 * 1024
        ),
    )(
        neighbours.T,
        counts,
        vis,
        delays.reshape(fac, pairs, 2, blk, lanes),
        tile_of,
        plane_of,
        kernels.reshape(planes * depth, cells),
    )
    spread = out.reshape(nz * groups, fac, NT_DEV, cells).astype(jnp.float32)
    return jnp.transpose(spread, (2, 1, 0, 3))


def solution(mesh):
    return jax.shard_map(
        local,
        mesh=mesh,
        in_specs=(
            P(None, None, None, ("facet", "chan"), None),
            P(),
            P("facet", None, None),
            P("facet", None),
            P("facet", None),
            P("facet"),
            P(),
        ),
        out_specs=P("chan", "facet", None, None),
        check_vma=False,
    )
```

profile of v0, /device:TPU:0, one launch (start us, length us, event | category | flops | bytes accessed | tf_op | source)
XLA Modules:
  0.0 35.8 jit_solution(561680089365606636)
XLA Ops:
  0.0 34.1 %shard_map.73 = bf16[4,1,32,512]{3,2,1,0:T(8,128)(2,1)} custom-call(s32[4,8]{1,0:T(4,128)} %bitcast.13, s32[2]{0:T(128)} %count_ref.1, bf16[2,8,4,2,32,128]{5,4,3,2,1,0:T(8,128)(2,1)} %bitcast.10, f32[2,4,2,32,128]{4,3,2,1,0:T(8,128)} %bitcast.12, s32[2,256]{1,0:T(2,128)} %tile_ref.1, s32[2,256]{1,0:T(2,128)} %plane_ref.1, bf16[8192,512]{1,0:T(8,128)(2,1)} %bitcast.9), custom_call_target="tpu_custom_call" | custom-call | tf_op jit(solution)/shard_map/pallas_call | solution.py:445
  34.1 1.7 %copy.10 = f32[4,2,16,512]{3,0,1,2:T(4,128)} copy(bf16[4,2,16,512]{3,2,1,0:T(8,128)(2,1)} %bitcast.11) | data formatting | bytes 393216 | tf_op jit(solution)/shard_map/transpose | solution.py:498
where the time goes:
time: 36 us; the launch traced here: 35.8 us
  Pallas kernels  34.1 us (95%)
  local copies, waits for them, and re-layouts  1.71 us (5%)
    pallas_call x1, Pallas kernels, local(): pl.pallas_call(functools.partial(kernel, cfg), out_shape=jax.ShapeDtypeSt...  34.1 us
    transpose x1, local copies, waits for them, and re-layouts, local(): return jnp.transpose(spread, (2, 1, 0, 3))  1.71 us

commit v1 on v0

v1 whole, which is shorter than its diff:
```python
import functools
import math

import jax
import jax.numpy as jnp
from jax import lax
from jax.experimental import pallas as pl
from jax.experimental.pallas import tpu as pltpu
from jax.sharding import PartitionSpec as P

AVG = 8
TS = 16
NT_DEV = 16
EDGE = 4
LANES = 128
JOINED = 3
ORDER = (3, 0, 1, 2)
FIRST = 2
MESH = pl.DeviceIdType.MESH


def series(first, count, scale):
    return [
        (-1.0) ** i * scale ** (2 * i + first) / math.factorial(2 * i + first)
        for i in range(count)
    ]


SIN_HALF = series(1, 7, math.pi)
COS_HALF = series(0, 7, math.pi)


def turn_parts(turns):
    frac = turns - jnp.round(turns)
    square = frac * frac
    sine = jnp.full_like(frac, SIN_HALF[-1])
    cosine = jnp.full_like(frac, COS_HALF[-1])
    for a, b in zip(SIN_HALF[-2::-1], COS_HALF[-2::-1]):
        sine = sine * square + a
        cosine = cosine * square + b
    sine = sine * frac
    return 1.0 - 2.0 * sine * sine, 2.0 * sine * cosine


def flip(index, mask):
    bit = 1
    while bit <= mask:
        if mask & bit:
            index = index + bit - 2 * bit * lax.rem(index // bit, 2)
        bit *= 2
    return index


def kernel(
    cfg,
    neigh_hbm,
    count_hbm,
    vis_ref,
    delay_ref,
    tile_hbm,
    plane_hbm,
    kern_ref,
    out_ref,
    neigh_ref,
    count_ref,
    tile_ref,
    plane_ref,
    pair,
    part,
    got,
    raw,
    wide,
    rough,
    low,
    turns,
    codes,
    rows,
    kern,
    lhs,
    grid,
    final,
    mate_send,
    mate_recv,
    rough_send,
    rough_recv,
    low_send,
    low_recv,
    turn_send,
    turn_recv,
    code_send,
    code_recv,
    part_send,
    part_recv,
    raw_send,
    raw_recv,
    row_send,
    row_recv,
    relay_send,
    relay_recv,
    fin_send,
    fin_recv,
    own_sem,
    small_sem,
):
    n, nz, facets, fac, blk, groups, planes, tiles, joined, order = cfg
    me = lax.axis_index("chan")
    zme = lax.axis_index("facet")
    channels = groups * AVG * nz
    tile = kern_ref.shape[1] // 2
    edge = EDGE * TS
    pairs = n // 2
    parity = lax.rem(me, 2)
    mate = me + 1 - 2 * parity
    my_pair = me // 2
    half_avg = AVG // 2
    blocks = blk * n
    chunk_z = [flip(zme, c) for c in range(nz)]
    far_first = list(range(nz - 1, 0, -1))

    def group_of(c):
        return pl.ds(chunk_z[c] * fac, fac)

    barrier = pltpu.get_barrier_semaphore()
    for d in range(1, n):
        pl.semaphore_signal(
            barrier, inc=1, device_id={"chan": lax.rem(me + d, n)}, device_id_type=MESH
        )
    for d in range(1, nz):
        pl.semaphore_signal(
            barrier, inc=1, device_id={"facet": chunk_z[d]}, device_id_type=MESH
        )

    def local_copy(src, dst, sem):
        return pltpu.make_async_copy(src, dst, sem)

    own_wide = local_copy(delay_ref.at[:, :, parity], wide, small_sem.at[0])
    small = [
        local_copy(tile_hbm, tile_ref, small_sem.at[1]),
        local_copy(plane_hbm, plane_ref, small_sem.at[2]),
        local_copy(count_hbm, count_ref, small_sem.at[3]),
        local_copy(neigh_hbm, neigh_ref, small_sem.at[4]),
    ]
    load_kern = local_copy(kern_ref, kern, small_sem.at[5])

    def own_copy(c):
        if c >= joined:
            return local_copy(
                vis_ref.at[:, group_of(c), my_pair, parity], raw.at[me, c - joined], own_sem.at[c]
            )
        return local_copy(
            vis_ref.at[:, group_of(c), :, parity], pair.at[parity, c], own_sem.at[c]
        )

    def chan_copy(src, dst, send, recv, peer):
        return pltpu.make_async_remote_copy(
            src_ref=src,
            dst_ref=dst,
            send_sem=send,
            recv_sem=recv,
            device_id={"chan": peer},
            device_id_type=MESH,
        )

    def facet_copy(src, dst, send, recv, c):
        return pltpu.make_async_remote_copy(
            src_ref=src,
            dst_ref=dst,
            send_sem=send,
            recv_sem=recv,
            device_id={"facet": chunk_z[c]},
            device_id_type=MESH,
        )

    own_wide.start()
    for copy in small:
        copy.start()
    for c in range(nz):
        own_copy(c).start()
    with jax.named_scope("barrier"):
        pl.semaphore_wait(barrier, n + nz - 2)

    def mate_copy(c, slot):
        return chan_copy(
            vis_ref.at[:, group_of(c), :, 1 - parity],
            pair.at[slot, c],
            mate_send,
            mate_recv.at[c],
            mate,
        )

    for c in range(joined):
        mate_copy(c, parity).start()
    for c in range(joined, nz):
        for m in range(n - 1, 0, -1):
            peer = flip(me, m)
            chan_copy(
                vis_ref.at[:, group_of(c), peer // 2, lax.rem(peer, 2)],
                raw.at[me, c - joined],
                raw_send,
                raw_recv.at[c - joined],
                peer,
            ).start()

    def rough_copy(c):
        return facet_copy(rough.at[0], rough.at[c], rough_send, rough_recv.at[c], c)

    def low_copy(c):
        return facet_copy(low.at[0], low.at[c], low_send, low_recv.at[c], c)

    def turn_copy(c):
        return facet_copy(
            wide.at[:, my_pair],
            turns.at[c - joined],
            turn_send,
            turn_recv.at[c - joined],
            c,
        )

    def code_copy(c):
        return facet_copy(codes.at[0], codes.at[c], code_send, code_recv.at[c], c)

    with jax.named_scope("delays"):
        own_wide.wait()
        rough[0] = wide[...].astype(jnp.bfloat16)
        for c in range(1, joined):
            rough_copy(c).start()
        mine = wide[:, my_pair]
        low[0] = (mine - mine.astype(jnp.bfloat16).astype(jnp.float32)).astype(jnp.bfloat16)
        for c in far_first:
            if c >= joined:
                turn_copy(c).start()
            else:
                low_copy(c).start()
    with jax.named_scope("codes"):
        for copy in small:
            copy.wait()
        block_id = lax.broadcasted_iota(jnp.int32, (1, blocks), 1)
        for i in range(fac):
            codes[0, i : i + 1] = jnp.where(
                block_id < count_ref[i],
                plane_ref[i : i + 1] * tiles + tile_ref[i : i + 1],
                -1,
            )
        for c in far_first:
            code_copy(c).start()

    def part_copy(c, peer, slot):
        return chan_copy(
            part.at[peer, c], got.at[slot, c], part_send, part_recv.at[c], 2 * peer + parity
        )

    def row_copy(c, peer):
        piece = rows.at[c, :, my_pair, parity]
        return chan_copy(piece, piece, row_send, row_recv.at[c], 2 * peer + parity)

    def relay_copy(c, side):
        piece = rows.at[c, :, :, side]
        return chan_copy(piece, piece, relay_send, relay_recv.at[c], mate)

    def join_pair(c):
        if c >= joined:
            return
        own_copy(c).wait()
        mate_copy(c, 1 - parity).wait_recv()
        if c:
            rough_copy(c).wait_recv()

        def one(i, carry):
            slot = i // pairs
            q = lax.rem(i, pairs)
            delay = rough[c, slot, q].astype(jnp.float32) if c else wide[slot, q]
            cosine, sine = turn_parts(delay * (0.5 / channels))
            real = pair[1, c, 0, slot, q].astype(jnp.float32)
            imag = pair[1, c, 1, slot, q].astype(jnp.float32)
            part[q, c, 0, slot] = (
                pair[0, c, 0, slot, q].astype(jnp.float32) + (real * cosine - imag * sine)
            ).astype(jnp.bfloat16)
            part[q, c, 1, slot] = (
                pair[0, c, 1, slot, q].astype(jnp.float32) + (real * sine + imag * cosine)
            ).astype(jnp.bfloat16)
            return carry

        lax.fori_loop(0, fac * pairs, one, 0)
        for m in range(pairs - 1, 0, -1):
            part_copy(c, flip(my_pair, m), my_pair).start()
        got[my_pair, c] = part[my_pair, c]

    def rotate(c):
        if c >= joined:
            turn_copy(c).wait_recv()
            own_copy(c).wait()
            every = raw.at[0 : n - 1, c - joined]
            chan_copy(every, every, raw_send, raw_recv.at[c - joined], mate).wait_recv()
            terms = AVG
        else:
            if c:
                low_copy(c).wait_recv()
            every = got.at[0 : pairs - 1, c]
            chan_copy(every, every, part_send, part_recv.at[c], mate).wait_recv()
            terms = half_avg
        step_turns = 0.5 * AVG / (terms * channels)

        def one(i, carry):
            if c >= joined:
                delay = turns[c - joined, i]
            elif c:
                delay = rough[c, i, my_pair].astype(jnp.float32) + low[c, i].astype(jnp.float32)
            else:
                delay = wide[i, my_pair]

            def term(k, p):
                block = raw[k, c - joined, p, i] if c >= joined else got[k, c, p, i]
                return block.astype(jnp.float32)

            step_cos, step_sin = turn_parts(delay * step_turns)
            for g in range(groups):
                first = (zme * groups + g) * AVG
                start_cos, start_sin = turn_parts(
                    delay * (1.0 + (0.5 / channels) * first.astype(jnp.float32))
                )
                top = (g + 1) * terms - 1
                real = term(top, 0)
                imag = term(top, 1)
                for k in range(top - 1, g * terms - 1, -1):
                    next_real = term(k, 0) + (real * step_cos - imag * step_sin)
                    imag = term(k, 1) + (real * step_sin + imag * step_cos)
                    real = next_real
                rows[c, i, my_pair, parity, :, 2 * LANES * g : 2 * LANES * g + LANES] = (
                    (real * start_cos - imag * start_sin) * (1.0 / AVG)
                ).astype(jnp.bfloat16)
                rows[c, i, my_pair, parity, :, 2 * LANES * g + LANES : 2 * LANES * (g + 1)] = (
                    (real * start_sin + imag * start_cos) * (1.0 / AVG)
                ).astype(jnp.bfloat16)
            return carry

        lax.fori_loop(0, fac, one, 0)
        for m in range(pairs - 1, 0, -1):
            row_copy(c, flip(my_pair, m)).start()

    def relay(c):
        every = rows.at[c, :, 0 : pairs - 1, 0]
        chan_copy(every, every, row_send, row_recv.at[c], mate).wait_recv()
        relay_copy(c, parity).start()

    entry = lax.broadcasted_iota(jnp.int32, (planes * NT_DEV, blocks), 0)
    wanted = (entry // NT_DEV) * tiles + me * NT_DEV + lax.rem(entry, NT_DEV)
    per_chunk = groups * fac * NT_DEV

    def gather_rows(c):
        if c:
            code_copy(c).wait_recv()
        relay_copy(c, 1 - parity).wait_recv()
        for i in range(fac):
            code = codes[c, i : i + 1]
            table = (code == wanted).astype(jnp.float32).astype(jnp.bfloat16)
            values = rows[c, i].reshape(blocks, rows.shape[-1])
            summed = jnp.dot(table, values, preferred_element_type=jnp.float32).astype(
                jnp.bfloat16
            )
            for g in range(groups):
                at = order.index(c) * per_chunk + (g * fac + i) * NT_DEV
                for p in range(planes):
                    lhs[at : at + NT_DEV, 2 * LANES * p : 2 * LANES * (p + 1)] = summed[
                        p * NT_DEV : (p + 1) * NT_DEV, 2 * LANES * g : 2 * LANES * (g + 1)
                    ]

    def fin_copy(c, first, width):
        columns = pl.ds(first, width)
        return facet_copy(
            final.at[c, :, :, columns], out_ref.at[zme, :, :, columns], fin_send, fin_recv, c
        )

    def put(c, first, width):
        at = order.index(c) * per_chunk
        for g in range(groups):
            here = at + g * fac * NT_DEV
            final[c, g, :, first : first + width] = grid[
                here : here + fac * NT_DEV, first : first + width
            ].astype(jnp.bfloat16)

    def multiply(top, bottom, first, width):
        grid[top:bottom, first : first + width] = jnp.dot(
            lhs[top:bottom],
            kern[:, first : first + width],
            preferred_element_type=jnp.float32,
        )

    span = nz * per_chunk
    early = FIRST * per_chunk

    def mm_first():
        load_kern.wait()
        multiply(0, early, 0, 2 * tile)
        for half in range(2):
            for c in far_first:
                if order.index(c) < FIRST:
                    put(c, half * tile, tile - LANES)
                    fin_copy(c, half * tile, tile - LANES).start()

    def blend_weights():
        row_id = lax.broadcasted_iota(jnp.int32, (NT_DEV, span), 0)
        col_id = lax.broadcasted_iota(jnp.int32, (NT_DEV, span), 1)
        same_tile = lax.rem(col_id, NT_DEV) == row_id
        slot = col_id // NT_DEV
        weights = []
        for c in order:
            for g in range(groups):
                for i in range(fac):
                    f = chunk_z[c] * fac + i
                    weight = jnp.zeros((NT_DEV, span), jnp.float32)
                    for k in range(neigh_ref.shape[0]):
                        other = neigh_ref[k, f]
                        there = jnp.zeros((NT_DEV, span), jnp.bool_)
                        for pos, b in enumerate(order):
                            base = (pos * groups + g) * fac
                            inside = (slot >= base) & (slot < base + fac)
                            there = there | (
                                inside & (slot - base + chunk_z[b] * fac == other)
                            )
                        weight += jnp.where(there & same_tile, 0.25, 0.0)
                    weights.append(weight)
        return jnp.concatenate(weights, axis=0).astype(jnp.bfloat16)

    keep = lax.broadcasted_iota(jnp.int32, (span, LANES), 1) >= LANES - edge

    runs = {
        "join": join_pair,
        "rotate": rotate,
        "relay": relay,
        "gather": gather_rows,
    }
    if nz == len(ORDER):
        plan = [
            ("join", 0),
            ("join", 1),
            ("join", 2),
            ("kern", 0),
            ("rotate", 3),
            ("rotate", 0),
            ("relay", 3),
            ("rotate", 1),
            ("relay", 0),
            ("gather", 3),
            ("rotate", 2),
            ("relay", 1),
            ("gather", 0),
            ("first", 0),
            ("relay", 2),
            ("gather", 1),
            ("gather", 2),
        ]
    else:
        plan = [(what, c) for what in ("join", "rotate", "relay") for c in order]
        plan += [("kern", 0)]
        plan += [("gather", c) for c in order]
        plan += [("first", 0)]
    for what, c in plan:
        with jax.named_scope(what + str(c)):
            if what == "kern":
                load_kern.start()
            elif what == "first":
                mm_first()
            else:
                runs[what](c)

    with jax.named_scope("weights"):
        mix = blend_weights()
    for half in range(2):
        left = half * tile
        with jax.named_scope("mm" + str(half)):
            multiply(early, span, left, tile)
        with jax.named_scope("blend" + str(half)):
            blended = jnp.dot(
                mix,
                grid[:, left : left + LANES].astype(jnp.bfloat16),
                preferred_element_type=jnp.float32,
            )
            moved = pltpu.roll(blended, LANES - edge, 1)
            grid[:, left + tile - LANES : left + tile] += jnp.where(keep, moved, 0.0)
            for c in far_first + [0]:
                begun = c and order.index(c) < FIRST
                first = left + tile - LANES if begun else left
                width = LANES if begun else tile
                put(c, first, width)
                if c:
                    fin_copy(c, first, width).start()

    own_out = local_copy(final.at[0], out_ref.at[zme], small_sem.at[6])
    own_out.start()
    with jax.named_scope("drain"):
        def sent(ref, sem):
            chan_copy(ref, ref, sem, sem, mate).wait_send()

        sent(pair.at[0, 0:joined], mate_send)
        sent(part.at[0 : pairs - 1, 0:joined], part_send)
        if joined < nz:
            sent(raw.at[0 : n - 1], raw_send)
            sent(turns, turn_send)
        sent(rows.at[:, :, 0 : pairs - 1, 0], row_send)
        sent(rows.at[:, :, :, 0], relay_send)
        if joined > 1:
            sent(rough.at[1:joined], rough_send)
            sent(low.at[1:joined], low_send)
        sent(codes.at[1:nz], code_send)
        sent(final.at[1:nz], fin_send)
    with jax.named_scope("finwait"):
        every = out_ref.at[0 : nz - 1]
        chan_copy(every, every, fin_send, fin_recv, mate).wait_recv()
    own_out.wait()


def local(visibilities, kernels, delays, tile_of, plane_of, counts, neighbours):
    n = lax.axis_size("chan")
    nz = lax.axis_size("facet")
    halves, facets, blocks, ch_dev, lanes = visibilities.shape
    planes, depth, cells = kernels.shape
    fac = facets // nz
    blk = blocks // n
    pairs = n // 2
    groups = n * ch_dev // AVG
    tiles = NT_DEV * n
    vis = visibilities.reshape(halves, facets, pairs, 2, blk, lanes)
    joined = min(JOINED, nz)
    order = ORDER if nz == len(ORDER) else tuple(range(nz))
    cfg = (n, nz, facets, fac, blk, groups, planes, tiles, joined, order)
    dma = pltpu.SemaphoreType.DMA
    raws = max(nz - joined, 1)
    span = groups * facets * NT_DEV
    anywhere = pl.BlockSpec(memory_space=pl.ANY)
    out = pl.pallas_call(
        functools.partial(kernel, cfg),
        out_shape=jax.ShapeDtypeStruct((nz, groups, fac * NT_DEV, cells), jnp.bfloat16),
        in_specs=[anywhere] * 7,
        out_specs=anywhere,
        scratch_shapes=[
            pltpu.SMEM((neighbours.shape[1], facets), jnp.int32),
            pltpu.SMEM((fac,), jnp.int32),
            pltpu.VMEM((fac, blocks), jnp.int32),
            pltpu.VMEM((fac, blocks), jnp.int32),
            pltpu.VMEM((2, joined, halves, fac, pairs, blk, lanes), jnp.bfloat16),
            pltpu.VMEM((pairs, joined, halves, fac, blk, lanes), jnp.bfloat16),
            pltpu.VMEM((pairs, joined, halves, fac, blk, lanes), jnp.bfloat16),
            pltpu.VMEM((n, raws, halves, fac, blk, lanes), jnp.bfloat16),
            pltpu.VMEM((fac, pairs, blk, lanes), jnp.float32),
            pltpu.VMEM((joined, fac, pairs, blk, lanes), jnp.bfloat16),
            pltpu.VMEM((joined, fac, blk, lanes), jnp.bfloat16),
            pltpu.VMEM((raws, fac, blk, lanes), jnp.float32),
            pltpu.VMEM((nz, fac, blocks), jnp.int32),
            pltpu.VMEM((nz, fac, pairs, 2, blk, groups * depth), jnp.bfloat16),
            pltpu.VMEM((planes * depth, cells), jnp.bfloat16),
            pltpu.VMEM((span, planes * depth), jnp.bfloat16),
            pltpu.VMEM((span, cells), jnp.float32),
            pltpu.VMEM((nz, groups, fac * NT_DEV, cells), jnp.bfloat16),
            dma,
            dma((joined,)),
            dma,
            dma((joined,)),
            dma,
            dma((joined,)),
            dma,
            dma((raws,)),
            dma,
            dma((nz,)),
            dma,
            dma((joined,)),
            dma,
            dma((raws,)),
            dma,
            dma((nz,)),
            dma,
            dma((nz,)),
            dma,
            dma,
            dma((nz,)),
            dma((7,)),
        ],
        compiler_params=pltpu.CompilerParams(
            collective_id=0, has_side_effects=True, vmem_limit_bytes=60 * 1024 * 1024
        ),
    )(
        neighbours.T,
        counts,
        vis,
        delays.reshape(fac, pairs, 2, blk, lanes),
        tile_of,
        plane_of,
        kernels.reshape(planes * depth, cells),
    )
    spread = out.reshape(nz * groups, fac, NT_DEV, cells).astype(jnp.float32)
    return jnp.transpose(spread, (2, 1, 0, 3))


def solution(mesh):
    return jax.shard_map(
        local,
        mesh=mesh,
        in_specs=(
            P(None, None, None, ("facet", "chan"), None),
            P(),
            P("facet", None, None),
            P("facet", None),
            P("facet", None),
            P("facet"),
            P(),
        ),
        out_specs=P("chan", "facet", None, None),
        check_vma=False,
    )
```

time: 36 us -> 32.2 us (0.89)
  Pallas kernels: 34.1 us -> 30.3 us
    pallas_call x1, Pallas kernels: 34.1 us -> 30.3 us  [local(): pl.pallas_call(functools.partial(kernel, cfg), out_shape=jax.ShapeDtypeSt...]
where the time goes in v1:
time: 32.2 us; the launch traced here: 32.1 us
  Pallas kernels  30.3 us (94%)
  local copies, waits for them, and re-layouts  1.71 us (5%)
    pallas_call x1, Pallas kernels, local(): pl.pallas_call(functools.partial(kernel, cfg), out_shape=jax.ShapeDtypeSt...  30.3 us
    transpose x1, local copies, waits for them, and re-layouts, local(): return jnp.transpose(spread, (2, 1, 0, 3))  1.71 us

profile of v1, /device:TPU:0, one launch (start us, length us, event | category | flops | bytes accessed | tf_op | source)
XLA Modules:
  0.0 32.1 jit_solution(8692355554005440155)
XLA Ops:
  0.0 30.3 %shard_map.73 = bf16[4,1,32,512]{3,2,1,0:T(8,128)(2,1)} custom-call(s32[4,8]{1,0:T(4,128)} %bitcast.13, s32[2]{0:T(128)} %count_hbm.1, bf16[2,8,4,2,32,128]{5,4,3,2,1,0:T(8,128)(2,1)} %bitcast.10, f32[2,4,2,32,128]{4,3,2,1,0:T(8,128)} %bitcast.12, s32[2,256]{1,0:T(2,128)} %tile_hbm.1, s32[2,256]{1,0:T(2,128)} %plane_hbm.1, bf16[8192,512]{1,0:T(8,128)(2,1)} %bitcast.9), custom_call_target="tpu_custom_call" | custom-call | tf_op jit(solution)/shard_map/pallas_call | solution.py:530
  30.4 1.7 %copy.10 = f32[4,2,16,512]{3,0,1,2:T(4,128)} copy(bf16[4,2,16,512]{3,2,1,0:T(8,128)(2,1)} %bitcast.11) | data formatting | bytes 393216 | tf_op jit(solution)/shard_map/transpose | solution.py:590
